TPU v7x, 128 devices: a whole 4x4x4 slice. The times are simulated.
128 devices in a mesh: row: 8 (over x, core), col: 16 (over z, y).
Axes of the slice: x: 4, y: 4, z: 4, core: 2. Of those that a mesh axis runs over, the one named last changes fastest.
Arguments:
- stored: float32 [16384, 16384], P('row', 'col'), as said below
Outputs:
- updated: float32 [16384, 16384], P('row', 'col')
- log_det: float32 [], replicated
Inputs may be any that keep to these rules, and one draw needn't show every extreme that they name: `stored`: read back into global order, the matrix is symmetric positive definite, with every eigenvalue at least 1.
All inputs are finite; a program needn't handle non-finite values.
Results may differ from a plain program's by a relative error of at most 0.0001.
Values sent between devices are 32-bit elements; how exact they have to be, the bound alone decides.
A program may use at most 256 MiB of HBM per device.

v0:
```python
import jax
import jax.numpy as jnp
from jax import lax
from jax.sharding import PartitionSpec as P

NB = 512
PANELS = 2


def from_root(value, axis, root):
    return lax.dynamic_index_in_dim(lax.all_gather(value, axis), root, 0, keepdims=False)


def from_root_2(value, axis, source):
    kept = jnp.where(lax.axis_index(axis) == source, value, 0).astype(value.dtype)
    return lax.psum(kept, axis)


def per_device(stored):
    row_count = lax.axis_size("row")
    col_count = lax.axis_size("col")
    row_index = lax.axis_index("row")
    col_index = lax.axis_index("col")
    local_rows, local_cols = stored.shape
    ratio = col_count // row_count
    col_blocks = local_cols // NB
    row_block = jnp.arange(local_rows, dtype=jnp.int32) // NB * row_count + row_index
    col_block = jnp.arange(local_cols, dtype=jnp.int32) // NB * col_count + col_index
    identity = jnp.eye(NB, dtype=jnp.float32)
    matrix = stored
    log_total = jnp.zeros((), jnp.float32)
    for number in range(PANELS):
        own_col = number // col_count
        own_row = number // row_count
        root_row = number % row_count
        root_col = number % col_count
        column_slab = matrix[:, own_col * NB : (own_col + 1) * NB]
        pivot_block = column_slab[own_row * NB : (own_row + 1) * NB]
        pivot_block = from_root(pivot_block, "row", root_row)
        factor = jnp.linalg.cholesky(pivot_block)
        inverse = jax.scipy.linalg.solve_triangular(factor, identity, lower=True)
        solved = jnp.dot(
            column_slab,
            inverse.T,
            precision=lax.Precision.HIGHEST,
            preferred_element_type=jnp.float32,
        )
        below_mask = (row_block > number)[:, None]
        at_mask = (row_block == number)[:, None]
        tiled = jnp.tile(factor, (local_rows // NB, 1))
        panel_full = jnp.where(below_mask, solved, jnp.where(at_mask, tiled, 0.0))
        log_term = 2.0 * jnp.sum(jnp.log(jnp.diagonal(factor)))
        panel_full = from_root_2(panel_full, "col", root_col)
        log_total = log_total + jnp.where(col_index == root_col, log_term, 0.0)
        picked = lax.dynamic_index_in_dim(
            panel_full.reshape(col_blocks, ratio, NB, NB), col_index // row_count, 1, keepdims=False
        )
        right_rows = from_root_2(picked.reshape(local_cols, NB), "row", col_index % row_count)
        left_rows = jnp.where(below_mask, panel_full, 0.0)
        right_rows = jnp.where((col_block > number)[:, None], right_rows, 0.0)
        matrix = matrix - jnp.dot(
            left_rows,
            right_rows.T,
            precision=lax.Precision.HIGHEST,
            preferred_element_type=jnp.float32,
        )
        old_column = matrix[:, own_col * NB : (own_col + 1) * NB]
        new_column = jnp.where(col_index == root_col, panel_full, old_column)
        matrix = matrix.at[:, own_col * NB : (own_col + 1) * NB].set(new_column)
        upper_mask = at_mask & (col_block > number)[None, :]
        matrix = jnp.where(upper_mask, 0.0, matrix)
    log_total = lax.psum(log_total, "col")
    return (matrix, log_total)


def solution(mesh):
    placed = (P("row", "col"),)
    return jax.shard_map(
        per_device, mesh=mesh, in_specs=placed, out_specs=(P("row", "col"), P()), check_vma=False
    )
```

profile of v0, /device:TPU:0, one launch (start us, length us, event | category | flops | bytes accessed | tf_op | source)
XLA Modules:
  0.0 887.8 jit_solution(12284626979522440874)
XLA Ops:
  7.2 9.1 %copy.16 = f32[2048,1024]{0,1:T(8,128)} copy(f32[2048,1024]{1,0:T(8,128)} %param.8) | data formatting | bytes 16777216 | tf_op args[0]
  18.9 52.1 %all-gather.5.cloned.1.call-done = f32[4096,512]{0,1:T(8,128)} async-done(((f32[512,512]{0,1:T(8,128)}), f32[4096,512]{0,1:T(8,128)}) %all-gather.5.cloned.1.call-update) | async-done | bytes 8388624 | tf_op jit(solution)/shard_map/all_gather | solution.py:11
  74.1 11.7 %cholesky.286 = f32[128,128]{1,0:T(8,128)S(1)} custom-call(f32[128,128]{1,0:T(8,128)S(1)} %cholesky.426), custom_call_target="Cholesky" | custom-call | tf_op jit(solution)/shard_map/jit(cholesky)/cholesky | solution.py:40
  85.9 9.8 %custom-call.31 = f32[1,128,128]{1,2,0:T(8,128)S(1)} custom-call(f32[1,128,128]{2,1,0:T(8,128)S(1)} %get-tuple-element.91), custom_call_target="InvertDiagBlocksLowerTriangular" | custom-call | tf_op jit(solution)/shard_map/jit(cholesky)/cholesky | solution.py:40
  98.3 11.7 %cholesky.305 = f32[128,128]{1,0:T(8,128)S(1)} custom-call(f32[128,128]{1,0:T(8,128)S(1)} %cholesky.430), custom_call_target="Cholesky" | custom-call | tf_op jit(solution)/shard_map/jit(cholesky)/cholesky | solution.py:40
  110.1 10.0 %custom-call.32 = f32[1,128,128]{1,2,0:T(8,128)S(1)} custom-call(f32[1,128,128]{2,1,0:T(8,128)S(1)} %get-tuple-element.88), custom_call_target="InvertDiagBlocksLowerTriangular" | custom-call | tf_op jit(solution)/shard_map/jit(cholesky)/cholesky | solution.py:40
  121.6 11.7 %cholesky.326 = f32[128,128]{1,0:T(8,128)S(1)} custom-call(f32[128,128]{1,0:T(8,128)S(1)} %cholesky.435), custom_call_target="Cholesky" | custom-call | tf_op jit(solution)/shard_map/jit(cholesky)/cholesky | solution.py:40
  134.1 9.8 %custom-call.33 = f32[1,128,128]{1,2,0:T(8,128)S(1)} custom-call(f32[1,128,128]{2,1,0:T(8,128)S(1)} %get-tuple-element.85), custom_call_target="InvertDiagBlocksLowerTriangular" | custom-call | tf_op jit(solution)/shard_map/jit(cholesky)/cholesky | solution.py:40
  145.3 11.7 %cholesky.343 = f32[128,128]{1,0:T(8,128)S(1)} custom-call(f32[128,128]{1,0:T(8,128)S(1)} %convolution_subtract_fusion.11), custom_call_target="Cholesky" | custom-call | tf_op jit(solution)/shard_map/jit(cholesky)/cholesky | solution.py:40
  162.6 12.0 %while.6 = (s32[]{:T(128)}, f32[512,512]{1,0:T(8,128)}, s32[4,2]{0,1:T(2,128)S(1)}, f32[4,128,128]{2,1,0:T(8,128)S(1)}, s32[]{:T(128)}) while((s32[]{:T(128)}, f32[512,512]{1,0:T(8,128)}, s32[4,2]{0,1:T(2,128)S(1)}, f32[4,128,128]{2,1,0:T(8,128)S(1)}, s32[]{:T(128)}) %tuple.69), condition=%wide.while_cond.2, body=%wide.while_body.2.sunk | while | flops 2 | bytes 131189 | solution.py:41
  174.6 39.3 %custom-call.34 = f32[4,128,128]{1,2,0:T(8,128)S(1)} custom-call(f32[4,128,128]{2,1,0:T(8,128)S(1)} %get-tuple-element.42), custom_call_target="InvertDiagBlocksLowerTriangular" | custom-call | tf_op jit(solution)/shard_map/jit(_solve_triangular)/triangular_solve | solution.py:41
  233.0 104.0 %all-reduce.6.cloned.1.call-done = f32[2048,512]{0,1:T(8,128)} async-done(((f32[2048,512]{0,1:T(8,128)}), f32[2048,512]{0,1:T(8,128)}) %all-reduce.6.cloned.1.call-update) | async-done | bytes 4194320 | tf_op jit(solution)/shard_map/psum | solution.py:16
  343.6 9.4 %fusion.21 = f32[2,512,512]{1,0,2:T(2,128)S(1)} fusion(pred[]{:T(512)S(6)} %eq.40, f32[2,2,512,512]{2,1,0,3:T(2,128)} %reshape.171, s32[]{:T(128)S(6)} %select_n.161), kind=kLoop, calls=%fused_computation.27 | loop fusion | flops 524288 | bytes 4194309 | tf_op jit(solution)/shard_map/jit(_where)/select_n | solution.py:15
  355.6 64.6 %all-reduce.8.cloned.1.call-done = f32[1024,512]{0,1:T(8,128)} async-done(((f32[1024,512]{0,1:T(8,128)}), f32[1024,512]{0,1:T(8,128)}) %all-reduce.8.cloned.1.call-update) | async-done | bytes 2097168 | tf_op jit(solution)/shard_map/psum | solution.py:16
  420.2 17.1 %fusion.11 = f32[2048,1024]{0,1:T(8,128)S(1)} fusion(f32[2048,1024]{0,1:T(8,128)} %copy.16, f32[2048,512]{0,1:T(8,128)} %all-reduce.6.cloned.1.call-done, f32[1024,512]{0,1:T(8,128)} %all-reduce.8.cloned.1.call-done, pred[2048]{0:T(1024)(128)(4,1)S(1)} %get-tuple-element.100, pred[1024]{0:T(1024)(128)(4,1)S(1)} %fusion.120), kind=kOutput, calls=%fused_computation.25 | convolution fusion | flops 12888571904 | bytes 23071744 | tf_op jit(solution)/shard_map/dot_general | solution.py:61
  445.3 48.9 %all-gather.7.cloned.1.call-done = f32[4096,512]{0,1:T(8,128)} async-done(((f32[512,512]{0,1:T(8,128)}), f32[4096,512]{0,1:T(8,128)}) %all-gather.7.cloned.1.call-update) | async-done | bytes 8388624 | tf_op jit(solution)/shard_map/all_gather | solution.py:11
  500.6 11.7 %cholesky.358 = f32[128,128]{1,0:T(8,128)S(1)} custom-call(f32[128,128]{1,0:T(8,128)S(1)} %cholesky.439), custom_call_target="Cholesky" | custom-call | tf_op jit(solution)/shard_map/jit(cholesky)/cholesky | solution.py:40
  513.0 9.8 %custom-call.35 = f32[1,128,128]{1,2,0:T(8,128)S(1)} custom-call(f32[1,128,128]{2,1,0:T(8,128)S(1)} %get-tuple-element.81), custom_call_target="InvertDiagBlocksLowerTriangular" | custom-call | tf_op jit(solution)/shard_map/jit(cholesky)/cholesky | solution.py:40
  525.4 11.7 %cholesky.377 = f32[128,128]{1,0:T(8,128)S(1)} custom-call(f32[128,128]{1,0:T(8,128)S(1)} %cholesky.443), custom_call_target="Cholesky" | custom-call | tf_op jit(solution)/shard_map/jit(cholesky)/cholesky | solution.py:40
  537.8 9.9 %custom-call.36 = f32[1,128,128]{1,2,0:T(8,128)S(1)} custom-call(f32[1,128,128]{2,1,0:T(8,128)S(1)} %get-tuple-element.78), custom_call_target="InvertDiagBlocksLowerTriangular" | custom-call | tf_op jit(solution)/shard_map/jit(cholesky)/cholesky | solution.py:40
  549.4 11.7 %cholesky.398 = f32[128,128]{1,0:T(8,128)S(1)} custom-call(f32[128,128]{1,0:T(8,128)S(1)} %cholesky.448), custom_call_target="Cholesky" | custom-call | tf_op jit(solution)/shard_map/jit(cholesky)/cholesky | solution.py:40
  561.8 9.8 %custom-call.37 = f32[1,128,128]{1,2,0:T(8,128)S(1)} custom-call(f32[1,128,128]{2,1,0:T(8,128)S(1)} %get-tuple-element.75), custom_call_target="InvertDiagBlocksLowerTriangular" | custom-call | tf_op jit(solution)/shard_map/jit(cholesky)/cholesky | solution.py:40
  573.0 11.7 %cholesky.415 = f32[128,128]{1,0:T(8,128)S(1)} custom-call(f32[128,128]{1,0:T(8,128)S(1)} %convolution_subtract_fusion.10), custom_call_target="Cholesky" | custom-call | tf_op jit(solution)/shard_map/jit(cholesky)/cholesky | solution.py:40
  590.8 11.5 %while.7 = (s32[]{:T(128)}, f32[512,512]{1,0:T(8,128)}, s32[4,2]{0,1:T(2,128)S(1)}, f32[4,128,128]{2,1,0:T(8,128)S(1)}, s32[]{:T(128)}) while((s32[]{:T(128)}, f32[512,512]{1,0:T(8,128)}, s32[4,2]{0,1:T(2,128)S(1)}, f32[4,128,128]{2,1,0:T(8,128)S(1)}, s32[]{:T(128)}) %tuple.87), condition=%wide.while_cond.2.clone, body=%wide.while_body.2.clone.sunk | while | flops 2 | bytes 131189 | solution.py:41
  603.0 40.1 %custom-call.38 = f32[4,128,128]{1,2,0:T(8,128)S(1)} custom-call(f32[4,128,128]{2,1,0:T(8,128)} %copy-done.8), custom_call_target="InvertDiagBlocksLowerTriangular" | custom-call | tf_op jit(solution)/shard_map/jit(_solve_triangular)/triangular_solve | solution.py:41
  652.1 8.5 select_select_fusion.2
  661.1 103.8 %all-reduce.10.cloned.1.call-done = f32[2048,512]{0,1:T(8,128)} async-done(((f32[2048,512]{0,1:T(8,128)}), f32[2048,512]{0,1:T(8,128)}) %all-reduce.10.cloned.1.call-update) | async-done | bytes 4194320 | tf_op jit(solution)/shard_map/psum | solution.py:16
  771.5 9.4 %fusion.22 = f32[2,512,512]{1,0,2:T(2,128)S(1)} fusion(pred[]{:T(512)S(6)} %eq.40, f32[2,2,512,512]{2,1,0,3:T(2,128)} %reshape.172, s32[]{:T(128)S(6)} %select_n.161), kind=kLoop, calls=%fused_computation.28 | loop fusion | flops 524288 | bytes 4194309 | tf_op jit(solution)/shard_map/jit(_where)/select_n | solution.py:15
  794.3 39.1 %psum.39 = f32[]{:T(128)} all-reduce(f32[]{:T(128)S(6)} %add.143), channel_id=1, replica_groups=mesh['row'=8,'col'=16] {'col'}, use_global_device_ids=true, to_apply=%region_15.18 | all-reduce | flops 1 | bytes 8 | tf_op jit(solution)/shard_map/psum | solution.py:72
  833.4 14.9 %all-reduce.12.cloned.1.call-done = f32[1024,512]{0,1:T(8,128)} async-done(((f32[1024,512]{0,1:T(8,128)}), f32[1024,512]{0,1:T(8,128)}) %all-reduce.12.cloned.1.call-update) | async-done | bytes 2097168 | tf_op jit(solution)/shard_map/psum | solution.py:16
  848.3 17.1 %fusion.14 = f32[2048,1024]{0,1:T(8,128)S(1)} fusion(f32[2048,1024]{0,1:T(8,128)} %copy-done, f32[2048,512]{0,1:T(8,128)} %all-reduce.10.cloned.1.call-done, f32[1024,512]{0,1:T(8,128)} %all-reduce.12.cloned.1.call-done, pred[2048]{0:T(1024)(128)(4,1)S(1)} %get-tuple-element.98, pred[1024]{0:T(1024)(128)(4,1)S(1)} %fusion.121), kind=kOutput, calls=%fused_computation.26 | convolution fusion | flops 12888571904 | bytes 23071744 | tf_op jit(solution)/shard_map/dot_general | solution.py:61
  871.5 9.2 %copy.22 = f32[2048,1024]{1,0:T(8,128)} copy(f32[2048,1024]{0,1:T(8,128)} %and_select_fusion.1) | data formatting | bytes 16777216
  (153 shorter events, 126.6 us)
Async XLA Ops:
  7.2 63.8 %all-gather.5.cloned.1.call-start = ((), (), s32[]{:S(2)}) async-start(), calls=%async_computation.4 | async-start | bytes 9437184 | tf_op jit(solution)/shard_map/all_gather | solution.py:11
  18.7 318.3 %all-reduce.6.cloned.1.call-start = ((), (), s32[]{:S(2)}) async-start(), calls=%async_computation | async-start | bytes 8388608 | tf_op jit(solution)/shard_map/psum | solution.py:16
  74.1 11.8 %copy-start.7 = (f32[512,512]{1,0:T(8,128)}, f32[512,512]{1,0:T(8,128)S(1)}, u32[]{:S(2)}) copy-start(f32[512,512]{1,0:T(8,128)S(1)} %fusion.44) | copy-start | bytes 3145732
  215.3 6.0 copy-start.5
  219.1 4.9 slice-start.2
  222.0 2.2 slice-start.3
  232.8 187.4 %all-reduce.8.cloned.1.call-start = ((), (), s32[]{:S(2)}) async-start(), calls=%async_computation.1 | async-start | bytes 4194304 | tf_op jit(solution)/shard_map/psum | solution.py:16
  354.8 139.4 %all-gather.7.cloned.1.call-start = ((), (), s32[]{:S(2)}) async-start(), calls=%async_computation.5 | async-start | bytes 9437184 | tf_op jit(solution)/shard_map/all_gather | solution.py:11
  420.2 17.2 %copy-start.1 = (f32[2048,512]{0,1:T(8,128)S(1)}, f32[2048,512]{0,1:T(8,128)}, u32[]{:S(2)}) copy-start(f32[2048,512]{0,1:T(8,128)} %all-reduce.6.cloned.1.call-done) | copy-start | bytes 12582916
  440.2 3.4 copy-start
  444.8 320.1 %all-reduce.10.cloned.1.call-start = ((), (), s32[]{:S(2)}) async-start(), calls=%async_computation.2 | async-start | bytes 8388608 | tf_op jit(solution)/shard_map/psum | solution.py:16
  499.6 1.0 copy-start.6
  584.8 3.5 copy-start.3
  602.3 0.7 copy-start.8
  643.2 6.0 copy-start.4
  647.0 4.9 slice-start
  649.9 2.2 slice-start.1
  660.7 187.6 %all-reduce.12.cloned.1.call-start = ((), (), s32[]{:S(2)}) async-start(), calls=%async_computation.3 | async-start | bytes 4194304 | tf_op jit(solution)/shard_map/psum | solution.py:16
  848.3 17.2 %copy-start.2 = (f32[2048,512]{0,1:T(8,128)S(1)}, f32[2048,512]{0,1:T(8,128)}, u32[]{:S(2)}) copy-start(f32[2048,512]{0,1:T(8,128)} %all-reduce.10.cloned.1.call-done) | copy-start | bytes 12582916
Sparse Core Ops, SparseCore 0:
  18.9 52.0 all-gather.4
  232.9 104.0 all-reduce.5
  354.9 65.2 all-reduce.7
  444.9 49.2 all-gather.6
  660.8 104.0 all-reduce.9
  782.8 65.3 all-reduce.11
where the time goes:
time: 898 us; the launch traced here: 888 us
  waiting for transfers between devices  388 us (43%)
  other arithmetic  273 us (30%)
  local copies, waits for them, and re-layouts  90.5 us (10%)
  matrix products  74.1 us (8%)
  blocking collectives  39.1 us (4%)
  between operations  21.5 us (2%)
    psum x4, waiting for transfers between devices, from_root_2(): return lax.psum(kept, axis)  287 us
    another operation x29, other arithmetic, per_device(): factor = jnp.linalg.cholesky(pivot_block)  158 us
    all_gather x2, waiting for transfers between devices, from_root(): lax.all_gather(value, axis)  101 us
    another operation x5, other arithmetic, per_device(): inverse = jax.scipy.linalg.solve_triangular(factor, identity, lower=True)  81.7 us
    psum x1, blocking collectives, per_device(): log_total = lax.psum(log_total, 'col')  39.1 us
    dot_general x2, matrix products, per_device(): jnp.dot(left_rows, right_rows.T, precision=lax.Precision.HIGHEST, preferr...  34.3 us
    unnamed x32, local copies, waits for them, and re-layouts  31.5 us
    another operation x27, local copies, waits for them, and re-layouts, per_device(): inverse = jax.scipy.linalg.solve_triangular(factor, identity, lower=True)  23.4 us
  transfers between devices with their start and end apart: 6, of which 6 were waited for; matrix products, arithmetic and copies ran while one was open for 1% of the time, Pallas kernels for 0%

commit v1 on v0

--- a/solution.py
+++ b/solution.py
@@ -13,7 +13,7 @@
 
 def from_root_2(value, axis, source):
     kept = jnp.where(lax.axis_index(axis) == source, value, 0).astype(value.dtype)
-    return lax.psum(kept, axis)
+    return jnp.sum(lax.all_gather(kept, axis), axis=0)
 
 
 def per_device(stored):

time: 898 us -> 1640 us (1.83)
  waiting for transfers between devices: 388 us -> 957 us
  local copies, waits for them, and re-layouts: 90.5 us -> 210 us
  other arithmetic: 273 us -> 329 us
    all_gather x0 -> x4, waiting for transfers between devices: none -> 855 us  [from_root_2(): return jnp.sum(lax.all_gather(kept, axis), axis=0)]
    psum x4 -> x0, waiting for transfers between devices: 287 us -> none  [from_root_2(): return lax.psum(kept, axis)]
    unnamed x32, local copies, waits for them, and re-layouts: 31.5 us -> 143 us
    reduce_sum x0 -> x4, other arithmetic: none -> 65.4 us  [from_root_2(): return jnp.sum(lax.all_gather(kept, axis), axis=0)]
where the time goes in v1:
time: 1640 us; the launch traced here: 1630 us
  waiting for transfers between devices  957 us (58%)
  other arithmetic  329 us (20%)
  local copies, waits for them, and re-layouts  210 us (13%)
  matrix products  69.2 us (4%)
  blocking collectives  39.3 us (2%)
  between operations  21.9 us (1%)
    all_gather x4, waiting for transfers between devices, from_root_2(): return jnp.sum(lax.all_gather(kept, axis), axis=0)  855 us
    another operation x29, other arithmetic, per_device(): factor = jnp.linalg.cholesky(pivot_block)  158 us
    unnamed x32, local copies, waits for them, and re-layouts  143 us
    all_gather x2, waiting for transfers between devices, from_root(): lax.all_gather(value, axis)  102 us
    another operation x5, other arithmetic, per_device(): inverse = jax.scipy.linalg.solve_triangular(factor, identity, lower=True)  81.8 us
    reduce_sum x4, other arithmetic, from_root_2(): return jnp.sum(lax.all_gather(kept, axis), axis=0)  65.4 us
    psum x1, blocking collectives, per_device(): log_total = lax.psum(log_total, 'col')  39.3 us
    dot_general x2, matrix products, per_device(): jnp.dot(left_rows, right_rows.T, precision=lax.Precision.HIGHEST, preferr...  33 us
  transfers between devices with their start and end apart: 6, of which 6 were waited for; matrix products, arithmetic and copies ran while one was open for 1% of the time, Pallas kernels for 0%

profile of v1, /device:TPU:0, one launch (start us, length us, event | category | flops | bytes accessed | tf_op | source)
XLA Modules:
  0.0 1628.1 jit_solution(2439249065153007164)
XLA Ops:
  18.9 52.1 %all-gather.15.cloned.1.call-done = f32[4096,512]{0,1:T(8,128)} async-done(((f32[512,512]{0,1:T(8,128)}), f32[4096,512]{0,1:T(8,128)}) %all-gather.15.cloned.1.call-update) | async-done | bytes 8388624 | tf_op jit(solution)/shard_map/all_gather | solution.py:11
  74.1 11.7 cholesky.286
  85.9 9.8 custom-call.31
  98.3 11.7 cholesky.305
  110.1 9.9 custom-call.32
  121.6 11.7 cholesky.326
  134.0 9.8 custom-call.33
  145.3 11.7 cholesky.343
  162.5 12.1 while.6
  174.6 39.3 %custom-call.34 = f32[4,128,128]{1,2,0:T(8,128)S(1)} custom-call(f32[4,128,128]{2,1,0:T(8,128)S(1)} %get-tuple-element.42), custom_call_target="InvertDiagBlocksLowerTriangular" | custom-call | tf_op jit(solution)/shard_map/jit(_solve_triangular)/triangular_solve | solution.py:41
  233.3 368.5 %all-gather.17.cloned.1.call-done = f32[32768,512]{0,1:T(8,128)} async-done(((f32[2048,512]{0,1:T(8,128)}), f32[32768,512]{0,1:T(8,128)}) %all-gather.17.cloned.1.call-update) | async-done | bytes 67108880 | tf_op jit(solution)/shard_map/all_gather | solution.py:16
  601.8 56.3 %copy.43 = f32[64,8,16,2048]{3,2,1,0:T(8,128)} copy(f32[64,8,16,2048]{3,1,2,0:T(8,128)} %bitcast.37) | data formatting | bytes 134217728
  658.1 23.3 %bitcast_reduce_fusion.1 = f32[2048,512]{0,1:T(8,128)} fusion(f32[64,8,16,2048]{3,2,1,0:T(8,128)} %copy.43), kind=kLoop, calls=%fused_computation.7 | loop fusion | flops 15728640 | bytes 71303168 | tf_op jit(solution)/shard_map/reduce_sum | solution.py:16
  697.7 83.7 %all-gather.11.cloned.1.call-done = f32[8,1024,512]{2,1,0:T(8,128)} async-done(((f32[1,1024,512]{2,1,0:T(8,128)}), f32[8,1024,512]{2,1,0:T(8,128)}) %all-gather.11.cloned.1.call-update) | async-done | bytes 16777232 | tf_op jit(solution)/shard_map/all_gather | solution.py:16
  781.4 9.4 reduce_sum.55
  792.8 16.5 %fusion.11 = f32[2048,1024]{0,1:T(8,128)S(1)} fusion(f32[2048,1024]{0,1:T(8,128)} %copy.28, f32[2048,512]{0,1:T(8,128)} %bitcast_reduce_fusion.1, f32[1024,512]{0,1:T(8,128)S(1)} %copy.40, pred[2048]{0:T(1024)(128)(4,1)S(1)} %get-tuple-element.102, pred[1024]{0:T(1024)(128)(4,1)S(1)} %fusion.118), kind=kOutput, calls=%fused_computation.27 | convolution fusion | flops 12888571904 | bytes 23071744 | tf_op jit(solution)/shard_map/dot_general | solution.py:61
  816.9 50.1 %all-gather.19.cloned.1.call-done = f32[4096,512]{0,1:T(8,128)} async-done(((f32[512,512]{0,1:T(8,128)}), f32[4096,512]{0,1:T(8,128)}) %all-gather.19.cloned.1.call-update) | async-done | bytes 8388624 | tf_op jit(solution)/shard_map/all_gather | solution.py:11
  870.1 11.7 cholesky.358
  882.5 9.8 custom-call.35
  893.1 11.7 cholesky.377
  905.5 10.2 custom-call.36
  916.4 11.7 cholesky.398
  928.8 9.8 custom-call.37
  939.2 11.7 cholesky.415
  955.8 12.0 while.7
  968.6 40.1 %custom-call.38 = f32[4,128,128]{1,2,0:T(8,128)S(1)} custom-call(f32[4,128,128]{2,1,0:T(8,128)} %copy-done.7), custom_call_target="InvertDiagBlocksLowerTriangular" | custom-call | tf_op jit(solution)/shard_map/jit(_solve_triangular)/triangular_solve | solution.py:41
  1026.4 368.8 %all-gather.21.cloned.1.call-done = f32[32768,512]{0,1:T(8,128)} async-done(((f32[2048,512]{0,1:T(8,128)}), f32[32768,512]{0,1:T(8,128)}) %all-gather.21.cloned.1.call-update) | async-done | bytes 67108880 | tf_op jit(solution)/shard_map/all_gather | solution.py:16
  1395.2 56.3 %copy.45 = f32[64,8,16,2048]{3,2,1,0:T(8,128)} copy(f32[64,8,16,2048]{3,1,2,0:T(8,128)} %bitcast.46) | data formatting | bytes 134217728
  1451.5 23.3 %bitcast_reduce_fusion = f32[2048,512]{0,1:T(8,128)} fusion(f32[64,8,16,2048]{3,2,1,0:T(8,128)} %copy.45), kind=kLoop, calls=%fused_computation.6 | loop fusion | flops 15728640 | bytes 71303168 | tf_op jit(solution)/shard_map/reduce_sum | solution.py:16
  1504.8 39.3 %psum.7 = f32[]{:T(128)} all-reduce(f32[]{:T(128)S(6)} %add.135), channel_id=1, replica_groups=mesh['row'=8,'col'=16] {'col'}, use_global_device_ids=true, to_apply=%region_15.18 | all-reduce | flops 1 | bytes 8 | tf_op jit(solution)/shard_map/psum | solution.py:72
  1544.1 33.7 %all-gather.13.cloned.1.call-done = f32[8,1024,512]{2,1,0:T(8,128)} async-done(((f32[1,1024,512]{2,1,0:T(8,128)}), f32[8,1024,512]{2,1,0:T(8,128)}) %all-gather.13.cloned.1.call-update) | async-done | bytes 16777232 | tf_op jit(solution)/shard_map/all_gather | solution.py:16
  1589.1 16.5 %fusion.14 = f32[2048,1024]{0,1:T(8,128)S(1)} fusion(f32[2048,1024]{0,1:T(8,128)} %copy-done, f32[2048,512]{0,1:T(8,128)} %bitcast_reduce_fusion, f32[1024,512]{0,1:T(8,128)S(1)} %copy.41, pred[2048]{0:T(1024)(128)(4,1)S(1)} %get-tuple-element.100, pred[1024]{0:T(1024)(128)(4,1)S(1)} %fusion.119), kind=kOutput, calls=%fused_computation.28 | convolution fusion | flops 12888571904 | bytes 23071744 | tf_op jit(solution)/shard_map/dot_general | solution.py:61
  (159 shorter events, 175.9 us)
Async XLA Ops:
  7.2 63.8 %all-gather.15.cloned.1.call-start = ((), (), s32[]{:S(2)}) async-start(), calls=%async_computation.2 | async-start | bytes 9437184 | tf_op jit(solution)/shard_map/all_gather | solution.py:11
  18.7 583.1 %all-gather.17.cloned.1.call-start = ((), (), s32[]{:S(2)}) async-start(), calls=%async_computation.3 | async-start | bytes 71303168 | tf_op jit(solution)/shard_map/all_gather | solution.py:16
  74.1 11.8 copy-start.6
  162.4 58.4 %copy-start.3 = (f32[512,512]{1,0:T(8,128)}, f32[512,512]{1,0:T(8,128)S(1)}, u32[]{:S(2)}) copy-start(f32[512,512]{1,0:T(8,128)S(1)} %get-tuple-element.69) | copy-start | bytes 3145732
  215.3 6.0 copy-start.5
  219.2 4.9 slice-start.2
  222.1 2.2 slice-start.3
  232.8 548.6 %all-gather.11.cloned.1.call-start = ((), (), s32[]{:S(2)}) async-start(), calls=%async_computation | async-start | bytes 18874368 | tf_op jit(solution)/shard_map/all_gather | solution.py:16
  696.8 170.1 %all-gather.19.cloned.1.call-start = ((), (), s32[]{:S(2)}) async-start(), calls=%async_computation.4 | async-start | bytes 9437184 | tf_op jit(solution)/shard_map/all_gather | solution.py:11
  792.8 16.5 %copy-start.2 = (f32[2048,512]{0,1:T(8,128)S(1)}, f32[2048,512]{0,1:T(8,128)}, u32[]{:S(2)}) copy-start(f32[2048,512]{0,1:T(8,128)} %bitcast_reduce_fusion.1) | copy-start | bytes 12582916
  812.0 3.4 copy-start
  816.6 578.6 %all-gather.21.cloned.1.call-start = ((), (), s32[]{:S(2)}) async-start(), calls=%async_computation.5 | async-start | bytes 71303168 | tf_op jit(solution)/shard_map/all_gather | solution.py:16
  967.8 0.7 copy-start.7
  1012.5 4.9 slice-start
  1015.4 2.2 slice-start.1
  1026.2 551.6 %all-gather.13.cloned.1.call-start = ((), (), s32[]{:S(2)}) async-start(), calls=%async_computation.1 | async-start | bytes 18874368 | tf_op jit(solution)/shard_map/all_gather | solution.py:16
  1487.1 6.2 copy-start.4
  1589.1 16.5 %copy-start.1 = (f32[2048,512]{0,1:T(8,128)S(1)}, f32[2048,512]{0,1:T(8,128)}, u32[]{:S(2)}) copy-start(f32[2048,512]{0,1:T(8,128)} %bitcast_reduce_fusion) | copy-start | bytes 12582916
Sparse Core Ops, SparseCore 0:
  18.9 52.0 all-gather.14
  232.9 368.8 all-gather.16
  697.0 84.4 all-gather.10
  816.7 50.2 all-gather.18
  1026.3 368.8 all-gather.20
  1493.3 84.4 all-gather.12
